TPU v7x, 32 devices: a whole 2x2x4 slice. The times are simulated.
32 devices in a mesh: blk: 8 (over z, x), order: 4 (over y, core).
Axes of the slice: x: 2, y: 2, z: 4, core: 2. Of those that a mesh axis runs over, the one named last changes fastest.
Arguments:
- field: float32 [16, 512, 4096], P(None, 'blk', 'order'), may hold values from -6 to 6
- ocean_mask: int32 [512, 4096], P('blk', 'order'), may hold values from 0 to 1, as said below
- plan: int32 [512], replicated, may hold values from 0 to 384, as said below
- legendre: bfloat16 [384, 1024, 1024], P('blk', 'order'), may hold values from -0.4375 to 0.4375
Outputs:
- coefficients: float32 [1024, 16, 2, 1024], P('blk', None, None, 'order')
Inputs may be any that keep to these rules, and one draw needn't show every extreme that they name: `ocean_mask`: exactly 128 cycles are all land, at the ends of the cycle order; every other cycle has an ocean point. plan is 384 exactly at the cycles that are all land, and names every slot below 384 once at the other cycles; slot p belongs to index p // 48 of blk; the cycles of one index of blk name at most 8 slots of one index, and in every draw some index of blk names exactly 8 slots of some index.
All inputs are finite; a program needn't handle non-finite values.
Results may differ from a plain program's by a relative error of at most 0.0029.
Values may be sent and summed in bfloat16 or wider, within the bound.
No kernel may reach another device: no remote copies, remote signals or barrier semaphores. Data moves between devices by JAX's collectives and lax.ppermute only.
A program may use at most 128 MiB of HBM per device.

v0:
```python
import math

import jax
import jax.numpy as jnp
from jax import lax
from jax.sharding import PartitionSpec as P

NLON = 4096
M = 1024


def twiddle(first, count):
    longitudes = first + jnp.arange(count, dtype=jnp.int32)
    orders = jnp.arange(M, dtype=jnp.int32)
    product = longitudes[:, None] * orders[None, :] % NLON
    angle = product.astype(jnp.float32) * (2.0 * math.pi / NLON)
    scale = 1.0 / math.sqrt(NLON)
    return jnp.stack([jnp.cos(angle) * scale, -jnp.sin(angle) * scale], axis=1)


def transform(values, table):
    return jnp.einsum("frn,ncm->frcm", values, table, precision=lax.Precision.HIGHEST)


def pack_cycles(masked, plan, slot_dev):
    n_blk = lax.axis_size("blk")
    own_index = lax.axis_index("blk")
    cycle_dev = masked.shape[1]
    cap = (cycle_dev + n_blk - 1) // n_blk
    grid = plan.reshape(n_blk, cycle_dev)
    owner = grid // slot_dev
    positions = jnp.arange(cycle_dev, dtype=jnp.int32)
    earlier = positions[None, :] < positions[:, None]
    same_owner = owner[:, :, None] == owner[:, None, :]
    rank = jnp.sum(same_owner & earlier[None], axis=2, dtype=jnp.int32)
    send_pos = owner * cap + rank
    local_pos = lax.dynamic_index_in_dim(send_pos, own_index, 0, keepdims=False)
    buffer_ids = jnp.arange(n_blk * cap, dtype=jnp.int32)
    send_onehot = (buffer_ids[:, None] == local_pos[None, :]).astype(jnp.float32)
    outgoing = jnp.einsum("qr,frn->fqn", send_onehot, masked, precision=lax.Precision.HIGHEST)
    arrived = lax.all_to_all(outgoing, "blk", split_axis=1, concat_axis=1, tiled=True)
    source_pos = (jnp.arange(n_blk, dtype=jnp.int32)[:, None] * cap + rank).reshape(-1)
    mine = (owner == own_index).reshape(-1)
    slot_local = (grid % slot_dev).reshape(-1)
    slot_ids = jnp.arange(slot_dev, dtype=jnp.int32)
    slot_onehot = ((slot_local[None, :] == slot_ids[:, None]) & mine[None, :]).astype(jnp.float32)
    source_onehot = (source_pos[:, None] == buffer_ids[None, :]).astype(jnp.float32)
    receive_map = jnp.dot(slot_onehot, source_onehot, precision=lax.Precision.HIGHEST)
    return jnp.einsum("pq,fqn->fpn", receive_map, arrived, precision=lax.Precision.HIGHEST)


def body(field, ocean_mask, plan, legendre):
    lon_local = field.shape[2]
    slot_dev = legendre.shape[0]
    masked = field * ocean_mask.astype(jnp.float32)[None]
    packed = pack_cycles(masked, plan, slot_dev)
    first = lax.axis_index("order") * lon_local
    terms = transform(packed, twiddle(first, lon_local))
    spectrum = lax.psum_scatter(terms, "order", scatter_dimension=3, tiled=True).astype(
        jnp.bfloat16
    )
    terms = jnp.einsum("pml,fpcm->lfcm", legendre, spectrum, preferred_element_type=jnp.float32)
    coefficients = lax.psum_scatter(terms, "blk", scatter_dimension=0, tiled=True)
    return coefficients


def solution(mesh):
    placed = (P(None, "blk", "order"), P("blk", "order"), P(), P("blk", "order", None))
    return jax.shard_map(
        body, mesh=mesh, in_specs=placed, out_specs=P("blk", None, None, "order"), check_vma=False
    )
```

profile of v0, /device:TPU:0, one launch (start us, length us, event | category | flops | bytes accessed | tf_op | source)
XLA Modules:
  0.0 815.6 jit_solution(1129262318180836919)
XLA Ops:
  6.6 0.7 fusion.31
  7.3 0.1 and.67
  7.3 0.1 div.20
  7.4 1.0 convert_element_type.26
  8.4 0.3 convert_reduce_fusion
  8.7 0.1 multiply_add_fusion
  8.8 5.5 fusion.19
  14.3 4.5 copy.9
  18.8 7.4 all-to-all-start
  26.2 0.0 reduce-scatter.3.cloned.1.call-start
  26.3 0.1 add.77
  26.4 0.3 convolution_bitcast_fusion
  26.6 19.0 %cosine_multiply_fusion = (f32[1024,1,1024]{2,0,1:T(8,128)}, f32[1024,1,1024]{2,0,1:T(8,128)}) fusion(s32[1024]{0:T(1024)S(1)} %iota_add_fusion), kind=kLoop, calls=%fused_computation.16 | loop fusion | flops 17825792 | bytes 8392704 | tf_op jit(solution)/shard_map/mul | solution.py:18
  45.7 73.8 %all-to-all-done = f32[16,64,1024]{2,0,1:T(8,128)} async-done(((f32[16,64,1024]{2,0,1:T(8,128)}), f32[16,64,1024]{2,0,1:T(8,128)}, u32[]{:S(2)}, u32[]{:S(2)}) %all-to-all-start) | async-done | bytes 4194336 | tf_op jit(solution)/shard_map/all_to_all | solution.py:41
  119.5 8.1 fusion.11
  127.7 23.8 %fusion.5 = f32[16,48,2,1024]{3,1,2,0:T(8,128)} fusion(f32[1024,1,1024]{2,0,1:T(8,128)} %get-tuple-element.11, f32[1024,1,1024]{2,0,1:T(8,128)S(1)} %copy-done, f32[16,1024,48]{1,2,0:T(8,128)S(1)} %fusion.11), kind=kOutput, calls=%fused_computation.4 | convolution fusion | flops 19329449984 | bytes 17825792 | tf_op jit(solution)/shard_map/frn,ncm->frcm/dot_general | solution.py:22
  151.5 0.0 reduce-scatter.3.cloned.1.call-update
  151.5 0.0 reduce-scatter.5.cloned.1.call-start
  151.6 57.1 %reduce-scatter.3.cloned.1.call-done = f32[16,48,2,256]{3,1,2,0:T(8,128)} async-done(((f32[16,48,2,1024]{3,1,2,0:T(8,128)}), f32[16,48,2,256]{3,1,2,0:T(8,128)}) %reduce-scatter.3.cloned.1.call-update) | async-done | bytes 1572880 | tf_op jit(solution)/shard_map/reduce_scatter | solution.py:59
  208.7 1.5 convert_element_type.29
  210.2 3.0 copy.11
  213.2 51.2 %fusion.2 = f32[1024,16,2,256]{0,1,2,3:T(8,128)} fusion(bf16[16,48,2,256]{1,0,2,3:T(8,128)(2,1)S(1)} %copy.11, bf16[48,256,1024,1]{2,1,0,3:T(8,128)(2,1)} %bitcast.24), kind=kOutput, calls=%fused_computation.2 | convolution fusion | flops 805306368 | bytes 59506688 | tf_op jit(solution)/shard_map/pml,fpcm->lfcm/dot_general | solution.py:62
  264.4 538.6 %reduce-scatter.5.cloned.1.call-done = f32[128,16,2,256]{0,1,2,3:T(8,128)} async-done(((f32[1024,16,2,256]{0,1,2,3:T(8,128)}), f32[128,16,2,256]{0,1,2,3:T(8,128)}) %reduce-scatter.5.cloned.1.call-update) | async-done | bytes 4194320 | tf_op jit(solution)/shard_map/reduce_scatter | solution.py:63
  803.0 5.8 copy.13
  (11 shorter events, 0.1 us)
Async XLA Ops:
  18.8 7.6 copy-start.1
  18.8 100.7 %all-to-all-start = ((f32[16,64,1024]{2,0,1:T(8,128)}), f32[16,64,1024]{2,0,1:T(8,128)}, u32[]{:S(2)}, u32[]{:S(2)}) async-start(f32[16,64,1024]{2,0,1:T(8,128)} %copy.9), calls=%async_computation | async-start | bytes 8388608 | tf_op jit(solution)/shard_map/all_to_all | solution.py:41
  26.2 182.4 %reduce-scatter.3.cloned.1.call-start = ((), (), s32[]{:S(2)}) async-start(), calls=%async_computation.3 | async-start | bytes 7864320 | tf_op jit(solution)/shard_map/reduce_scatter | solution.py:59
  119.5 8.2 copy-start
  151.5 651.5 %reduce-scatter.5.cloned.1.call-start = ((), (), s32[]{:S(2)}) async-start(), calls=%async_computation.4 | async-start | bytes 37748736 | tf_op jit(solution)/shard_map/reduce_scatter | solution.py:63
Sparse Core Ops, SparseCore 0:
  151.7 56.9 reduce-scatter.2
  264.5 538.4 reduce-scatter.4
where the time goes:
time: 816 us
  waiting for transfers between devices  670 us (82%)
  matrix products  88.9 us (11%)
  other arithmetic  22.6 us (3%)
  local copies, waits for them, and re-layouts  13.6 us (2%)
  between operations  13.5 us (2%)
    reduce_scatter x1, waiting for transfers between devices, body(): lax.psum_scatter(terms, 'blk', scatter_dimension=0, tiled=True)  539 us
    all_to_all x1, waiting for transfers between devices, pack_cycles(): lax.all_to_all(outgoing, 'blk', split_axis=1, concat_axis=1, tiled=True)  73.8 us
    reduce_scatter x1, waiting for transfers between devices, body(): lax.psum_scatter(terms, 'order', scatter_dimension=3, tiled=True)  57.1 us
    dot_general x1, matrix products, body(): jnp.einsum('pml,fpcm->lfcm', legendre, spectrum, preferred_element_type=j...  51.2 us
    dot_general x1, matrix products, transform(): jnp.einsum('frn,ncm->frcm', values, table, precision=lax.Precision.HIGHEST)  23.8 us
    mul x1, other arithmetic, twiddle(): return jnp.stack([jnp.cos(angle) * scale, -jnp.sin(angle) * scale], axis=1)  19 us
  transfers between devices with their start and end apart: 3, of which 3 were waited for; matrix products, arithmetic and copies ran while one was open for 2% of the time, Pallas kernels for 0%

commit v1 on v0

v1 whole, which is shorter than its diff:
```python
import functools
import math

import jax
import jax.numpy as jnp
from jax import lax
from jax.experimental import pallas as pl
from jax.experimental.pallas import tpu as pltpu
from jax.sharding import PartitionSpec as P

NLON = 4096
M = 1024
GROUP = 16
CHUNKS = 8


def trig(product, period):
    angle = (product % period).astype(jnp.float32) * (2.0 * math.pi / period)
    return jnp.cos(angle), jnp.sin(angle)


def spectrum_of(rows):
    quarter = NLON // 4
    x = [rows[:, j * quarter : (j + 1) * quarter] for j in range(4)]
    even, odd = x[0] + x[2], x[1] + x[3]
    d, t = x[0] - x[2], x[1] - x[3]
    n = jnp.arange(quarter, dtype=jnp.int32)
    scale = 1.0 / math.sqrt(NLON)
    (c1, s1), (c2, s2), (c3, s3) = [[v[None] * scale for v in trig(r * n, NLON)] for r in (1, 2, 3)]
    both, diff = (even + odd) * scale, even - odd
    real = [both, d * c1 - t * s1, diff * c2, d * c3 + t * s3]
    imag = [jnp.zeros_like(both), -d * s1 - t * c1, -diff * s2, t * c3 - d * s3]
    z = jnp.stack([jnp.concatenate([a, b], axis=1) for a, b in zip(real, imag)])
    k = jnp.arange(M // 4, dtype=jnp.int32)
    c, s = trig(n[:, None] * k[None, :], quarter)
    table = jnp.concatenate([jnp.concatenate([c, -s], axis=1), jnp.concatenate([s, c], axis=1)], axis=0)
    out = lax.dot_general(
        table, z, (((0,), (2,)), ((), ())), precision=lax.Precision.HIGH, preferred_element_type=jnp.float32
    )
    return out.astype(jnp.bfloat16).reshape(2, M, rows.shape[0])


def plan_maps(plan, slot_dev, cycle_dev):
    n_blk = lax.axis_size("blk")
    own = lax.axis_index("blk")
    cap = (cycle_dev + n_blk - 1) // n_blk
    grid = plan.reshape(n_blk, cycle_dev)
    owner = grid // slot_dev
    positions = jnp.arange(cycle_dev, dtype=jnp.int32)
    earlier = positions[None, :] < positions[:, None]
    same_owner = owner[:, :, None] == owner[:, None, :]
    rank = jnp.sum(same_owner & earlier[None], axis=2, dtype=jnp.int32)
    send_pos = owner * cap + rank
    local_pos = lax.dynamic_index_in_dim(send_pos, own, 0, keepdims=False)
    buffer_ids = jnp.arange(n_blk * cap, dtype=jnp.int32)
    send = (buffer_ids[:, None] == local_pos[None, :]).astype(jnp.bfloat16)
    source_pos = (jnp.arange(n_blk, dtype=jnp.int32)[:, None] * cap + rank).reshape(-1)
    mine = (owner == own).reshape(-1)
    slot_local = (grid % slot_dev).reshape(-1)
    slot_ids = jnp.arange(slot_dev, dtype=jnp.int32)
    slot_onehot = ((slot_local[None, :] == slot_ids[:, None]) & mine[None, :]).astype(jnp.bfloat16)
    source_onehot = (source_pos[:, None] == buffer_ids[None, :]).astype(jnp.bfloat16)
    receive = jnp.dot(slot_onehot, source_onehot, preferred_element_type=jnp.float32)
    return send, receive.astype(jnp.bfloat16)


def legendre_kernel(slots, fc, n_blk, bit_ref, table_ref, spec_ref, keep_ref, send_ref):
    depth = slots * GROUP
    spec = spec_ref[0].astype(jnp.float32)
    column = lax.broadcasted_iota(jnp.int32, (GROUP, depth), 1) % GROUP
    row = lax.broadcasted_iota(jnp.int32, (GROUP, depth), 0)
    diagonal = jnp.where(column == row, 1.0, 0.0)
    left = (spec[:, None, :] * diagonal[None]).reshape(fc * GROUP, depth).astype(jnp.bfloat16)
    table = table_ref[...].reshape(depth, table_ref.shape[2])
    out = jnp.dot(left, table, preferred_element_type=jnp.float32)
    width = out.shape[1] // n_blk
    odd = bit_ref[0] == 1
    for pair in range(n_blk // 2):
        low = out[:, 2 * pair * width : (2 * pair + 1) * width]
        high = out[:, (2 * pair + 1) * width : (2 * pair + 2) * width]
        keep_ref[pair, 0] = jnp.where(odd, high, low)
        send_ref[pair, 0] = jnp.where(odd, low, high).astype(jnp.bfloat16)


def contributions(legendre, spec, bit, first, count):
    slots, _, degrees = legendre.shape
    fc = spec.shape[1]
    n_blk = lax.axis_size("blk")
    width = degrees // n_blk
    shape = (n_blk // 2, count, fc * GROUP, width)
    block = pl.BlockSpec((n_blk // 2, 1, fc * GROUP, width), lambda i: (0, i, 0, 0))
    return pl.pallas_call(
        functools.partial(legendre_kernel, slots, fc, n_blk),
        grid=(count,),
        in_specs=[
            pl.BlockSpec(memory_space=pltpu.SMEM),
            pl.BlockSpec((slots, GROUP, degrees), lambda i: (0, first + i, 0)),
            pl.BlockSpec((1, fc, slots * GROUP), lambda i: (first + i, 0, 0)),
        ],
        out_specs=[block, block],
        out_shape=[jax.ShapeDtypeStruct(shape, jnp.float32), jax.ShapeDtypeStruct(shape, jnp.bfloat16)],
        cost_estimate=pl.CostEstimate(
            flops=2 * count * fc * GROUP * slots * GROUP * degrees,
            bytes_accessed=count * GROUP * degrees * (2 * slots + 3 * fc),
            transcendentals=0,
        ),
        name="legendre_terms",
    )(bit, legendre, spec)


def body(field, ocean_mask, plan, legendre):
    fields, cycle_dev, _ = field.shape
    slot_dev, orders, degrees = legendre.shape
    n_blk = lax.axis_size("blk")
    masked = field * ocean_mask.astype(jnp.float32)[None]
    whole = lax.all_to_all(masked, "order", split_axis=1, concat_axis=2, tiled=True)
    rows = whole.reshape(-1, NLON)
    spectrum = spectrum_of(rows).reshape(2, M, fields, -1)
    spectrum = lax.all_to_all(spectrum, "order", split_axis=1, concat_axis=3, tiled=True)
    send, receive = plan_maps(plan, slot_dev, cycle_dev)
    outgoing = jnp.einsum("qr,cmfr->qfcm", send, spectrum, preferred_element_type=jnp.float32)
    arrived = lax.all_to_all(
        outgoing.astype(jnp.bfloat16), "blk", split_axis=0, concat_axis=0, tiled=True
    )
    packed = jnp.einsum("pq,qfcm->fcpm", receive, arrived, preferred_element_type=jnp.float32)
    packed = packed.astype(jnp.bfloat16).reshape(fields * 2, slot_dev, orders // GROUP, GROUP)
    packed = packed.transpose(2, 0, 1, 3).reshape(orders // GROUP, fields * 2, slot_dev * GROUP)
    groups = orders // GROUP
    step = max(groups // CHUNKS, 1)
    bit = (lax.axis_index("blk") % 2).astype(jnp.int32).reshape(1)
    swap = [(i, i ^ 1) for i in range(n_blk)]
    alike = [[i for i in range(n_blk) if i % 2 == parity] for parity in range(2)]
    pieces = []
    for first in range(0, groups, step):
        keep, send = contributions(legendre, packed, bit, first, step)
        got = lax.ppermute(send, "blk", swap)
        terms = (keep + got.astype(jnp.float32)).astype(jnp.bfloat16)
        terms = lax.all_to_all(
            terms, "blk", split_axis=0, concat_axis=0, axis_index_groups=alike, tiled=True
        )
        pieces.append(jnp.sum(terms.astype(jnp.float32), axis=0))
    total = jnp.concatenate(pieces, axis=0)
    width = degrees // n_blk
    total = total.reshape(groups, fields, 2, GROUP, width)
    return total.transpose(4, 1, 2, 0, 3).reshape(width, fields, 2, orders)


def solution(mesh):
    placed = (P(None, "blk", "order"), P("blk", "order"), P(), P("blk", "order", None))
    return jax.shard_map(
        body, mesh=mesh, in_specs=placed, out_specs=P("blk", None, None, "order"), check_vma=False
    )
```

time: 816 us -> 493 us (0.60)
  waiting for transfers between devices: 670 us -> 241 us
  matrix products: 88.9 us -> 8.94 us
  local copies, waits for them, and re-layouts: 13.6 us -> 84.9 us
  starting transfers between devices: 7.5 us -> 65 us
  Pallas kernels: 0 us -> 36.6 us
  other arithmetic: 22.6 us -> 51.5 us
  between operations: 13.5 us -> 0.47 us
    reduce_scatter x2 -> x0, waiting for transfers between devices: 596 us -> none  [the longest x1 539 us: body(): lax.psum_scatter(terms, 'blk', scatter_dimension=0, tiled=True)]
    ppermute x0 -> x8, waiting for transfers between devices: none -> 146 us  [body(): got = lax.ppermute(send, 'blk', swap)]
    dot_general x5 -> x3, matrix products: 88.9 us -> 8.94 us  [the longest x1 7.5 us: spectrum_of(): lax.dot_general(table, z, (((0,), (2,)), ((), ())), precision=lax.Precisi...]
    all_to_all x1 -> x11, starting transfers between devices: 7.42 us -> 53.2 us  [the longest x8 37.2 us: body(): lax.all_to_all(terms, 'blk', split_axis=0, concat_axis=0, axis_index_grou...]
    pallas_call x0 -> x8, Pallas kernels: none -> 36.6 us  [contributions(): pl.pallas_call(functools.partial(legendre_kernel, slots, fc, n_blk), grid...]
    unnamed x4 -> x12, local copies, waits for them, and re-layouts: 0.01 us -> 29.9 us
    convert_element_type x1 -> x8, other arithmetic: 1.5 us -> 23.2 us  [body(): terms = (keep + got.astype(jnp.float32)).astype(jnp.bfloat16)]
    all_to_all x1 -> x11, waiting for transfers between devices: 73.8 us -> 94.7 us  [the longest x1 39.9 us: body(): lax.all_to_all(masked, 'order', split_axis=1, concat_axis=2, tiled=True)]
  transfers between devices with their start and end apart: 3 -> 19, of which waited for: 3 -> 13; matrix products, arithmetic and copies ran while one was open for 2% -> 9% of each run, Pallas kernels for 0% -> 7%
where the time goes in v1:
time: 493 us; the launch traced here: 488 us
  waiting for transfers between devices  241 us (49%)
  local copies, waits for them, and re-layouts  84.9 us (17%)
  starting transfers between devices  65 us (13%)
  other arithmetic  51.5 us (10%)
  Pallas kernels  36.6 us (7%)
  matrix products  8.94 us (2%)
    ppermute x8, waiting for transfers between devices, body(): got = lax.ppermute(send, 'blk', swap)  146 us
    all_to_all x1, waiting for transfers between devices, body(): lax.all_to_all(masked, 'order', split_axis=1, concat_axis=2, tiled=True)  39.9 us
    all_to_all x8, starting transfers between devices, body(): lax.all_to_all(terms, 'blk', split_axis=0, concat_axis=0, axis_index_grou...  37.2 us
    pallas_call x8, Pallas kernels, contributions(): pl.pallas_call(functools.partial(legendre_kernel, slots, fc, n_blk), grid...  36.6 us
    unnamed x12, local copies, waits for them, and re-layouts  29.9 us
    all_to_all x1, waiting for transfers between devices, body(): lax.all_to_all(outgoing.astype(jnp.bfloat16), 'blk', split_axis=0, concat...  25.4 us
    convert_element_type x8, other arithmetic, body(): terms = (keep + got.astype(jnp.float32)).astype(jnp.bfloat16)  23.2 us
    another operation x2, local copies, waits for them, and re-layouts, body(): spectrum = spectrum_of(rows).reshape(2, M, fields, -1)  15.6 us
  transfers between devices with their start and end apart: 19, of which 13 were waited for; matrix products, arithmetic and copies ran while one was open for 9% of the time, Pallas kernels for 7%

profile of v1, /device:TPU:0, one launch (start us, length us, event | category | flops | bytes accessed | tf_op | source)
XLA Modules:
  0.0 488.3 jit_solution(16614769077489020668)
XLA Ops:
  1.0 6.6 %copy_multiply_fusion = f32[16,64,1024]{2,0,1:T(8,128)} fusion(f32[16,64,1024]{2,1,0:T(8,128)} %param.4, f32[64,1024]{1,0:T(8,128)S(1)} %convert_element_type.153), kind=kLoop, calls=%fused_computation.15 | loop fusion | flops 1048576 | bytes 8650752 | tf_op jit(solution)/shard_map/mul | solution.py:115
  7.6 5.5 %all-to-all-start = ((f32[16,64,1024]{2,0,1:T(8,128)}), f32[16,64,1024]{2,0,1:T(8,128)}, u32[]{:S(2)}, u32[]{:S(2)}) async-start(f32[16,64,1024]{2,0,1:T(8,128)} %copy_multiply_fusion), calls=%async_computation | async-start | bytes 8388608 | tf_op jit(solution)/shard_map/all_to_all | solution.py:116
  21.6 39.9 %all-to-all-done = f32[16,64,1024]{2,0,1:T(8,128)} async-done(((f32[16,64,1024]{2,0,1:T(8,128)}), f32[16,64,1024]{2,0,1:T(8,128)}, u32[]{:S(2)}, u32[]{:S(2)}) %all-to-all-start) | async-done | bytes 4194336 | tf_op jit(solution)/shard_map/all_to_all | solution.py:116
  73.3 7.5 %fusion.14 = bf16[512,4,256]{2,0,1:T(8,128)(2,1)S(1)} fusion(f32[1,256,2048]{2,1,0:T(8,128)S(1)} %get-tuple-element.55, f32[1,256,2048]{2,1,0:T(8,128)S(1)} %get-tuple-element.54, f32[1,256,2048]{2,1,0:T(8,128)S(1)} %get-tuple-element.53, f32[1,256,2048]{2,1,0:T(8,128)S(1)} %get-tuple-element.56, f32[1024,256]{0,1:T(8,128)S(1)} %get-tuple-element.58, ...), kind=kOutput, calls=%fused_computation.39 | convolution fusion | flops 6452412416 | bytes 12582912 | tf_op jit(solution)/shard_map/dot_general | solution.py:37
  81.6 7.5 %reshape_reshape.3 = bf16[2,1024,16,16]{3,2,1,0:T(8,128)(2,1)} reshape(bf16[512,4,256]{2,1,0:T(4,128)(2,1)S(1)} %copy.64) | data formatting | bytes 2097152 | tf_op jit(solution)/shard_map/reshape;reshape | solution.py:118
  89.1 8.1 %copy.91 = bf16[2,1024,16,16]{3,2,0,1:T(8,128)(2,1)} copy(bf16[2,1024,16,16]{3,2,1,0:T(8,128)(2,1)} %reshape_reshape.3) | data formatting | bytes 2097152 | tf_op jit(solution)/shard_map/reshape;reshape | solution.py:118
  97.2 10.9 %reshape.191 = bf16[4,2,65536]{2,1,0:T(2,128)(2,1)} reshape(bf16[1024,2,16,16]{3,2,1,0:T(8,128)(2,1)} %bitcast.54) | data formatting | bytes 2097152
  112.0 14.0 %all-to-all-done.1 = bf16[4,2,65536]{2,1,0:T(2,128)(2,1)S(1)} async-done(((bf16[4,2,65536]{2,1,0:T(2,128)(2,1)}), bf16[4,2,65536]{2,1,0:T(2,128)(2,1)S(1)}, u32[]{:S(2)}, u32[]{:S(2)}) %all-to-all-start.1) | async-done | bytes 1048608 | tf_op jit(solution)/shard_map/all_to_all | solution.py:119
  126.0 7.1 %reshape.192 = bf16[1024,2,16,16]{3,2,1,0:T(8,128)(2,1)} reshape(bf16[4,2,65536]{2,1,0:T(2,128)(2,1)S(1)} %all-to-all-done.1) | data formatting | bytes 2097152
  133.1 9.2 %copy.84 = bf16[2,4,256,16,16]{2,1,4,3,0:T(4,128)(2,1)S(1)} copy(bf16[2,4,256,16,16]{4,3,0,2,1:T(8,128)(2,1)} %bitcast.53) | data formatting | bytes 2097152 | tf_op jit(solution)/shard_map/all_to_all | solution.py:119
  145.0 7.0 %all-to-all-start.2 = ((bf16[64,16,2,256]{3,2,1,0:T(2,128)(2,1)}), bf16[64,16,2,256]{3,2,1,0:T(2,128)(2,1)S(1)}, u32[]{:S(2)}, u32[]{:S(2)}) async-start(bf16[64,16,2,256]{3,2,1,0:T(2,128)(2,1)} %copy.69), calls=%async_computation.2 | async-start | bytes 2097152 | tf_op jit(solution)/shard_map/all_to_all | solution.py:122
  152.1 25.4 %all-to-all-done.2 = bf16[64,16,2,256]{3,2,1,0:T(2,128)(2,1)S(1)} async-done(((bf16[64,16,2,256]{3,2,1,0:T(2,128)(2,1)}), bf16[64,16,2,256]{3,2,1,0:T(2,128)(2,1)S(1)}, u32[]{:S(2)}, u32[]{:S(2)}) %all-to-all-start.2) | async-done | bytes 1048608 | tf_op jit(solution)/shard_map/all_to_all | solution.py:122
  180.3 5.3 %copy.72 = bf16[16,32,48,16]{1,3,2,0:T(8,128)(2,1)S(1)} copy(bf16[16,32,48,16]{2,3,0,1:T(8,128)(2,1)} %bitcast.58) | data formatting | bytes 1572864 | tf_op jit(solution)/shard_map/transpose | solution.py:127
  193.8 22.6 %collective-permute-done.6 = bf16[4,2,512,128]{3,2,1,0:T(8,128)(2,1)S(1)} collective-permute-done((bf16[4,2,512,128]{3,2,1,0:T(8,128)(2,1)}, bf16[4,2,512,128]{3,2,1,0:T(8,128)(2,1)S(1)}, u32[]{:S(2)}, u32[]{:S(2)}) %collective-permute-start.6) | collective-permute-done | bytes 1048608 | tf_op jit(solution)/shard_map/ppermute | solution.py:136
  229.3 22.4 %collective-permute-done.5 = bf16[4,2,512,128]{3,2,1,0:T(8,128)(2,1)S(1)} collective-permute-done((bf16[4,2,512,128]{3,2,1,0:T(8,128)(2,1)}, bf16[4,2,512,128]{3,2,1,0:T(8,128)(2,1)S(1)}, u32[]{:S(2)}, u32[]{:S(2)}) %collective-permute-start.5) | collective-permute-done | bytes 1048608 | tf_op jit(solution)/shard_map/ppermute | solution.py:136
  265.7 21.0 %collective-permute-done.4 = bf16[4,2,512,128]{3,2,1,0:T(8,128)(2,1)S(1)} collective-permute-done((bf16[4,2,512,128]{3,2,1,0:T(8,128)(2,1)}, bf16[4,2,512,128]{3,2,1,0:T(8,128)(2,1)S(1)}, u32[]{:S(2)}, u32[]{:S(2)}) %collective-permute-start.4) | collective-permute-done | bytes 1048608 | tf_op jit(solution)/shard_map/ppermute | solution.py:136
  300.6 19.6 %collective-permute-done.3 = bf16[4,2,512,128]{3,2,1,0:T(8,128)(2,1)S(1)} collective-permute-done((bf16[4,2,512,128]{3,2,1,0:T(8,128)(2,1)}, bf16[4,2,512,128]{3,2,1,0:T(8,128)(2,1)S(1)}, u32[]{:S(2)}, u32[]{:S(2)}) %collective-permute-start.3) | collective-permute-done | bytes 1048608 | tf_op jit(solution)/shard_map/ppermute | solution.py:136
  334.2 18.3 %collective-permute-done.1 = bf16[4,2,512,128]{3,2,1,0:T(8,128)(2,1)S(1)} collective-permute-done((bf16[4,2,512,128]{3,2,1,0:T(8,128)(2,1)}, bf16[4,2,512,128]{3,2,1,0:T(8,128)(2,1)S(1)}, u32[]{:S(2)}, u32[]{:S(2)}) %collective-permute-start.1) | collective-permute-done | bytes 1048608 | tf_op jit(solution)/shard_map/ppermute | solution.py:136
  366.3 17.0 %collective-permute-done = bf16[4,2,512,128]{3,2,1,0:T(8,128)(2,1)S(1)} collective-permute-done((bf16[4,2,512,128]{3,2,1,0:T(8,128)(2,1)}, bf16[4,2,512,128]{3,2,1,0:T(8,128)(2,1)S(1)}, u32[]{:S(2)}, u32[]{:S(2)}) %collective-permute-start) | collective-permute-done | bytes 1048608 | tf_op jit(solution)/shard_map/ppermute | solution.py:136
  402.4 19.7 %collective-permute-done.2 = bf16[4,2,512,128]{3,2,1,0:T(8,128)(2,1)} collective-permute-done((bf16[4,2,512,128]{3,2,1,0:T(8,128)(2,1)}, bf16[4,2,512,128]{3,2,1,0:T(8,128)(2,1)}, u32[]{:S(2)}, u32[]{:S(2)}) %collective-permute-start.2) | collective-permute-done | bytes 1048608 | tf_op jit(solution)/shard_map/ppermute | solution.py:136
  425.3 5.1 %all-to-all-start.5 = ((bf16[4,2,512,128]{3,2,1,0:T(8,128)(2,1)}), bf16[4,2,512,128]{3,2,1,0:T(8,128)(2,1)}, u32[]{:S(2)}, u32[]{:S(2)}) async-start(bf16[4,2,512,128]{3,2,1,0:T(8,128)(2,1)} %add_convert_fusion.5), calls=%async_computation.5 | async-start | bytes 2097152 | tf_op jit(solution)/shard_map/all_to_all | solution.py:138
  430.4 5.3 %collective-permute-done.7 = bf16[4,2,512,128]{3,2,1,0:T(8,128)(2,1)} collective-permute-done((bf16[4,2,512,128]{3,2,1,0:T(8,128)(2,1)}, bf16[4,2,512,128]{3,2,1,0:T(8,128)(2,1)}, u32[]{:S(2)}, u32[]{:S(2)}) %collective-permute-start.7) | collective-permute-done | bytes 1048608 | tf_op jit(solution)/shard_map/ppermute | solution.py:136
  443.2 10.5 %all-to-all-done.5 = bf16[4,2,512,128]{3,2,1,0:T(8,128)(2,1)} async-done(((bf16[4,2,512,128]{3,2,1,0:T(8,128)(2,1)}), bf16[4,2,512,128]{3,2,1,0:T(8,128)(2,1)}, u32[]{:S(2)}, u32[]{:S(2)}) %all-to-all-start.5) | async-done | bytes 1048608 | tf_op jit(solution)/shard_map/all_to_all | solution.py:138
  480.9 7.2 %copy.82 = f32[128,16,2,256]{3,2,1,0:T(2,128)} copy(f32[128,16,2,256]{0,3,2,1:T(8,128)} %bitcast.56) | data formatting | bytes 8388608 | tf_op jit(solution)/shard_map/reshape | solution.py:145
  (92 shorter events, 164.8 us)
Async XLA Ops:
  7.6 5.5 %copy-start = (s32[512]{0:T(512)S(1)}, s32[512]{0:T(512)}, u32[]{:S(2)}) copy-start(s32[512]{0:T(512)} %param.6) | copy-start | bytes 6148
  7.6 53.9 %all-to-all-start = ((f32[16,64,1024]{2,0,1:T(8,128)}), f32[16,64,1024]{2,0,1:T(8,128)}, u32[]{:S(2)}, u32[]{:S(2)}) async-start(f32[16,64,1024]{2,0,1:T(8,128)} %copy_multiply_fusion), calls=%async_computation | async-start | bytes 8388608 | tf_op jit(solution)/shard_map/all_to_all | solution.py:116
  108.1 17.9 %all-to-all-start.1 = ((bf16[4,2,65536]{2,1,0:T(2,128)(2,1)}), bf16[4,2,65536]{2,1,0:T(2,128)(2,1)S(1)}, u32[]{:S(2)}, u32[]{:S(2)}) async-start(bf16[4,2,65536]{2,1,0:T(2,128)(2,1)} %reshape.191), calls=%async_computation.1 | async-start | bytes 2097152 | tf_op jit(solution)/shard_map/all_to_all | solution.py:119
  145.0 32.6 %all-to-all-start.2 = ((bf16[64,16,2,256]{3,2,1,0:T(2,128)(2,1)}), bf16[64,16,2,256]{3,2,1,0:T(2,128)(2,1)S(1)}, u32[]{:S(2)}, u32[]{:S(2)}) async-start(bf16[64,16,2,256]{3,2,1,0:T(2,128)(2,1)} %copy.69), calls=%async_computation.2 | async-start | bytes 2097152 | tf_op jit(solution)/shard_map/all_to_all | solution.py:122
  192.5 23.9 %collective-permute-start.6 = (bf16[4,2,512,128]{3,2,1,0:T(8,128)(2,1)}, bf16[4,2,512,128]{3,2,1,0:T(8,128)(2,1)S(1)}, u32[]{:S(2)}, u32[]{:S(2)}) collective-permute-start(bf16[4,2,512,128]{3,2,1,0:T(8,128)(2,1)} %get-tuple-element.34), channel_id=1, source_target_pairs={{0,4},{4,0},{8,12},{12,8},{16,20},{20,16},{24,28},{28,24},{1,5},{5... | collective-permute-start | bytes 3145736 | tf_op jit(solution)/shard_map/ppermute | solution.py:136
  219.3 35.2 %all-to-all-start.9 = ((bf16[4,2,512,128]{3,2,1,0:T(8,128)(2,1)}), bf16[4,2,512,128]{3,2,1,0:T(8,128)(2,1)S(1)}, u32[]{:S(2)}, u32[]{:S(2)}) async-start(bf16[4,2,512,128]{3,2,1,0:T(8,128)(2,1)} %add_convert_fusion.1), calls=%async_computation.9 | async-start | bytes 2097152 | tf_op jit(solution)/shard_map/all_to_all | solution.py:138
  227.5 24.2 %collective-permute-start.5 = (bf16[4,2,512,128]{3,2,1,0:T(8,128)(2,1)}, bf16[4,2,512,128]{3,2,1,0:T(8,128)(2,1)S(1)}, u32[]{:S(2)}, u32[]{:S(2)}) collective-permute-start(bf16[4,2,512,128]{3,2,1,0:T(8,128)(2,1)} %get-tuple-element.32), channel_id=1, source_target_pairs={{0,4},{4,0},{8,12},{12,8},{16,20},{20,16},{24,28},{28,24},{1,5},{5... | collective-permute-start | bytes 3145736 | tf_op jit(solution)/shard_map/ppermute | solution.py:136
  254.5 35.0 %all-to-all-start.8 = ((bf16[4,2,512,128]{3,2,1,0:T(8,128)(2,1)}), bf16[4,2,512,128]{3,2,1,0:T(8,128)(2,1)S(1)}, u32[]{:S(2)}, u32[]{:S(2)}) async-start(bf16[4,2,512,128]{3,2,1,0:T(8,128)(2,1)} %add_convert_fusion.2), calls=%async_computation.8 | async-start | bytes 2097152 | tf_op jit(solution)/shard_map/all_to_all | solution.py:138
  263.9 22.8 %collective-permute-start.4 = (bf16[4,2,512,128]{3,2,1,0:T(8,128)(2,1)}, bf16[4,2,512,128]{3,2,1,0:T(8,128)(2,1)S(1)}, u32[]{:S(2)}, u32[]{:S(2)}) collective-permute-start(bf16[4,2,512,128]{3,2,1,0:T(8,128)(2,1)} %get-tuple-element.30), channel_id=1, source_target_pairs={{0,4},{4,0},{8,12},{12,8},{16,20},{20,16},{24,28},{28,24},{1,5},{5... | collective-permute-start | bytes 3145736 | tf_op jit(solution)/shard_map/ppermute | solution.py:136
  289.5 33.6 %all-to-all-start.7 = ((bf16[4,2,512,128]{3,2,1,0:T(8,128)(2,1)}), bf16[4,2,512,128]{3,2,1,0:T(8,128)(2,1)S(1)}, u32[]{:S(2)}, u32[]{:S(2)}) async-start(bf16[4,2,512,128]{3,2,1,0:T(8,128)(2,1)} %add_convert_fusion.3), calls=%async_computation.7 | async-start | bytes 2097152 | tf_op jit(solution)/shard_map/all_to_all | solution.py:138
  298.9 21.4 %collective-permute-start.3 = (bf16[4,2,512,128]{3,2,1,0:T(8,128)(2,1)}, bf16[4,2,512,128]{3,2,1,0:T(8,128)(2,1)S(1)}, u32[]{:S(2)}, u32[]{:S(2)}) collective-permute-start(bf16[4,2,512,128]{3,2,1,0:T(8,128)(2,1)} %get-tuple-element.28), channel_id=1, source_target_pairs={{0,4},{4,0},{8,12},{12,8},{16,20},{20,16},{24,28},{28,24},{1,5},{5... | collective-permute-start | bytes 3145736 | tf_op jit(solution)/shard_map/ppermute | solution.py:136
  323.1 32.2 %all-to-all-start.6 = ((bf16[4,2,512,128]{3,2,1,0:T(8,128)(2,1)}), bf16[4,2,512,128]{3,2,1,0:T(8,128)(2,1)}, u32[]{:S(2)}, u32[]{:S(2)}) async-start(bf16[4,2,512,128]{3,2,1,0:T(8,128)(2,1)} %add_convert_fusion.4), calls=%async_computation.6 | async-start | bytes 2097152 | tf_op jit(solution)/shard_map/all_to_all | solution.py:138
  332.5 20.0 %collective-permute-start.1 = (bf16[4,2,512,128]{3,2,1,0:T(8,128)(2,1)}, bf16[4,2,512,128]{3,2,1,0:T(8,128)(2,1)S(1)}, u32[]{:S(2)}, u32[]{:S(2)}) collective-permute-start(bf16[4,2,512,128]{3,2,1,0:T(8,128)(2,1)} %get-tuple-element.24), channel_id=1, source_target_pairs={{0,4},{4,0},{8,12},{12,8},{16,20},{20,16},{24,28},{28,24},{1,5},{5... | collective-permute-start | bytes 3145736 | tf_op jit(solution)/shard_map/ppermute | solution.py:136
  355.3 30.9 %all-to-all-start.4 = ((bf16[4,2,512,128]{3,2,1,0:T(8,128)(2,1)}), bf16[4,2,512,128]{3,2,1,0:T(8,128)(2,1)}, u32[]{:S(2)}, u32[]{:S(2)}) async-start(bf16[4,2,512,128]{3,2,1,0:T(8,128)(2,1)} %add_convert_fusion.6), calls=%async_computation.4 | async-start | bytes 2097152 | tf_op jit(solution)/shard_map/all_to_all | solution.py:138
  364.7 18.7 %collective-permute-start = (bf16[4,2,512,128]{3,2,1,0:T(8,128)(2,1)}, bf16[4,2,512,128]{3,2,1,0:T(8,128)(2,1)S(1)}, u32[]{:S(2)}, u32[]{:S(2)}) collective-permute-start(bf16[4,2,512,128]{3,2,1,0:T(8,128)(2,1)} %get-tuple-element.22), channel_id=1, source_target_pairs={{0,4},{4,0},{8,12},{12,8},{16,20},{20,16},{24,28},{28,24},{1,5},{5... | collective-permute-start | bytes 3145736 | tf_op jit(solution)/shard_map/ppermute | solution.py:136
  386.2 39.1 %all-to-all-start.3 = ((bf16[4,2,512,128]{3,2,1,0:T(8,128)(2,1)}), bf16[4,2,512,128]{3,2,1,0:T(8,128)(2,1)}, u32[]{:S(2)}, u32[]{:S(2)}) async-start(bf16[4,2,512,128]{3,2,1,0:T(8,128)(2,1)} %add_convert_fusion.7), calls=%async_computation.3 | async-start | bytes 2097152 | tf_op jit(solution)/shard_map/all_to_all | solution.py:138
  395.8 26.3 %collective-permute-start.2 = (bf16[4,2,512,128]{3,2,1,0:T(8,128)(2,1)}, bf16[4,2,512,128]{3,2,1,0:T(8,128)(2,1)}, u32[]{:S(2)}, u32[]{:S(2)}) collective-permute-start(bf16[4,2,512,128]{3,2,1,0:T(8,128)(2,1)} %get-tuple-element.26), channel_id=1, source_target_pairs={{0,4},{4,0},{8,12},{12,8},{16,20},{20,16},{24,28},{28,24},{1,5},{5... | collective-permute-start | bytes 3145736 | tf_op jit(solution)/shard_map/ppermute | solution.py:136
  402.0 33.7 %collective-permute-start.7 = (bf16[4,2,512,128]{3,2,1,0:T(8,128)(2,1)}, bf16[4,2,512,128]{3,2,1,0:T(8,128)(2,1)}, u32[]{:S(2)}, u32[]{:S(2)}) collective-permute-start(bf16[4,2,512,128]{3,2,1,0:T(8,128)(2,1)} %get-tuple-element.36), channel_id=1, source_target_pairs={{0,4},{4,0},{8,12},{12,8},{16,20},{20,16},{24,28},{28,24},{1,5},{5... | collective-permute-start | bytes 3145736 | tf_op jit(solution)/shard_map/ppermute | solution.py:136
  425.3 28.5 %all-to-all-start.5 = ((bf16[4,2,512,128]{3,2,1,0:T(8,128)(2,1)}), bf16[4,2,512,128]{3,2,1,0:T(8,128)(2,1)}, u32[]{:S(2)}, u32[]{:S(2)}) async-start(bf16[4,2,512,128]{3,2,1,0:T(8,128)(2,1)} %add_convert_fusion.5), calls=%async_computation.5 | async-start | bytes 2097152 | tf_op jit(solution)/shard_map/all_to_all | solution.py:138
  453.7 20.2 %all-to-all-start.10 = ((bf16[4,2,512,128]{3,2,1,0:T(8,128)(2,1)}), bf16[4,2,512,128]{3,2,1,0:T(8,128)(2,1)}, u32[]{:S(2)}, u32[]{:S(2)}) async-start(bf16[4,2,512,128]{3,2,1,0:T(8,128)(2,1)} %add_convert_fusion), calls=%async_computation.10 | async-start | bytes 2097152 | tf_op jit(solution)/shard_map/all_to_all | solution.py:138
